TPU v7x, 256 devices: a whole 4x4x8 slice. The times are simulated.
256 devices in a mesh: beam: 16 (over x_hi, y, core), tm: 16 (over z, x_lo).
Axes of the slice: x: 4 (x_hi: 2, x_lo: 2; x = x_hi * 2 + x_lo), y: 4, z: 8, core: 2. Of those that a mesh axis runs over, the one named last changes fastest.
Arguments:
- samples: float32 [2, 150994944], P(None, ('beam', 'tm')), parts along dimension 1, may hold values from -6 to 6
- prototype: float32 [16, 4096], replicated, may hold values from -1.5 to 1.5
Outputs:
- spectra: bfloat16 [2, 49152, 4096], P(None, 'beam', 'tm'), parts along dimension 1
There are 16 independent parts, one for each index of `beam`. A program takes and returns all parts, laid end to end along the dimension named above; an argument that names none is the same for every part. Nothing has to cross between parts.
All inputs are finite; a program needn't handle non-finite values.
Results may differ from a plain program's by a relative error of at most 0.001.
Values may be sent and summed in bfloat16 or wider, within the bound.
A program may use at most 128 MiB of HBM per device.

v0:
```python
import math

import jax
import jax.numpy as jnp
import numpy as np
from jax import lax
from jax.experimental import pallas as pl
from jax.experimental.pallas import tpu as pltpu
from jax.sharding import PartitionSpec as P

CHANNELS = 4096
TAPS = 16
HOP = 3072
LANES = 128
ROWS = 32
PEERS = 16
FRAME_ROWS = 2 * ROWS
HOP_ROWS = 2 * HOP // LANES
RIM_ROWS = 2 * (TAPS * CHANNELS - HOP) // LANES
STEP = 16
MESH = pl.DeviceIdType.MESH
OFFSETS = [(dz, dx) for dz in (1, -1, 2, -2, 3, -3, 4) for dx in (0, 1)] + [(0, 1)]


def split_bf16(table):
    high = table.astype(np.float32).astype(jnp.bfloat16)
    low = (table - high.astype(np.float64)).astype(np.float32).astype(jnp.bfloat16)
    return high, low


def first_matrix():
    a = np.arange(ROWS)
    table = np.zeros((2, 4, ROWS, 4, ROWS, 2))
    for frame in range(4):
        turns = (-np.outer(a, a) + 8 * a[:, None] * (frame + 1)) % 32
        unit = np.exp(2j * np.pi * turns / 32) / 64
        table[0, frame, :, frame, :, 0] = unit.real
        table[0, frame, :, frame, :, 1] = -unit.imag
        table[1, frame, :, frame, :, 0] = unit.imag
        table[1, frame, :, frame, :, 1] = unit.real
    return split_bf16(table.reshape(256, 256))


def middle_tables():
    turns = np.outer(np.arange(ROWS), np.arange(LANES))
    angle = 2 * np.pi * turns / CHANNELS
    tables = np.stack([np.cos(angle), np.sin(angle)])
    return np.tile(tables, (1, 4, 1)).reshape(256, LANES).astype(np.float32)


def second_matrix():
    k_l = (8 * np.arange(16)[None, :] + np.arange(8)[:, None]).reshape(-1)
    angle = 2 * np.pi * (np.outer(k_l, np.arange(LANES)) % LANES) / LANES
    c, s = np.cos(angle), np.sin(angle)
    return split_bf16(np.block([[c, s], [-s, c]]))


def peer(me, dz, dx):
    return (me // 2 + dz + 8) % 8 * 2 + (me % 2 + dx) % 2


def dot3(left_high, left_low, right_high, right_low, dims):
    def one(a, b):
        return lax.dot_general(a, b, (dims, ((), ())), preferred_element_type=jnp.float32)

    return one(left_high, right_high) + one(left_high, right_low) + one(left_low, right_high)


def halves(value):
    high = value.astype(jnp.bfloat16)
    return high, (value - high.astype(jnp.float32)).astype(jnp.bfloat16)


def kernel(
    frames, x_hbm, h_hbm, one_hbm, mid_hbm, two_hbm, o_ref,
    x, h, one, mid, two, fold_high, fold_low, turn_high, turn_low, staged, ready,
    load_sem, rim_sem, send_sem, recv_sem,
):
    me = lax.axis_index("tm")
    local_rows = frames * HOP_ROWS
    steps = frames // STEP
    first_step = 2
    low_row = first_step * STEP * HOP_ROWS - RIM_ROWS
    high_row = ((first_step + 1) * STEP - 1) * HOP_ROWS + TAPS * FRAME_ROWS - RIM_ROWS

    barrier = pltpu.get_barrier_semaphore()
    for dz, dx in OFFSETS:
        pl.semaphore_signal(barrier, inc=1, device_id={"tm": peer(me, dz, dx)}, device_id_type=MESH)

    def load(index, start, stop):
        return pltpu.make_async_copy(
            x_hbm.at[pl.ds(start, stop - start)], x.at[pl.ds(RIM_ROWS + start, stop - start)], load_sem.at[index]
        )

    early = [
        load(0, low_row, high_row),
        pltpu.make_async_copy(h_hbm, h, load_sem.at[3]),
        pltpu.make_async_copy(one_hbm, one, load_sem.at[4]),
        pltpu.make_async_copy(mid_hbm, mid, load_sem.at[5]),
        pltpu.make_async_copy(two_hbm, two, load_sem.at[6]),
    ]
    late = [load(1, high_row, local_rows), load(2, 0, low_row)]
    for copy in early + late:
        copy.start()

    pl.semaphore_wait(barrier, len(OFFSETS))

    def rim_copy():
        return pltpu.make_async_remote_copy(
            x_hbm.at[pl.ds(local_rows - RIM_ROWS, RIM_ROWS)],
            x.at[pl.ds(0, RIM_ROWS)],
            rim_sem.at[0],
            rim_sem.at[1],
            device_id={"tm": lax.rem(me + 1, PEERS)},
            device_id_type=MESH,
        )

    @pl.when(me < PEERS - 1)
    def _():
        rim_copy().start()

    @pl.when(me == 0)
    def _():
        x[pl.ds(0, RIM_ROWS), :] = jnp.zeros((RIM_ROWS, LANES), jnp.float32)

    for copy in early:
        copy.wait()

    lane = lax.broadcasted_iota(jnp.int32, (16, LANES), 1)
    low_64 = lane < 64
    even_32 = lane // 32 % 2 == 0

    def exchange(tiles):
        a, b, c, d = tiles
        ac = jnp.where(low_64, a, pltpu.roll(c, 64, 1)), jnp.where(low_64, pltpu.roll(a, 64, 1), c)
        bd = jnp.where(low_64, b, pltpu.roll(d, 64, 1)), jnp.where(low_64, pltpu.roll(b, 64, 1), d)
        done = []
        for p, q in zip(ac, bd):
            done.append(jnp.where(even_32, p, pltpu.roll(q, 32, 1)))
            done.append(jnp.where(even_32, pltpu.roll(p, 96, 1), q))
        return done

    def eight_frames(first_frame, sub):
        base = first_frame * HOP_ROWS

        def fold(block, carry):
            at = pl.multiple_of(block * 16, 16)
            taps = [h[pl.ds(at + p * FRAME_ROWS, 16), :] for p in range(TAPS)]
            for f in range(8):
                total = None
                for p in range(TAPS):
                    rows = pl.ds(pl.multiple_of(base + f * HOP_ROWS + p * FRAME_ROWS + at, 16), 16)
                    term = taps[p] * x[rows, :]
                    total = term if total is None else total + term
                high, low = halves(total)
                place = pl.ds(pl.multiple_of(f % 4 * FRAME_ROWS + at, 16), 16)
                fold_high[place, f // 4 * LANES : (f // 4 + 1) * LANES] = high
                fold_low[place, f // 4 * LANES : (f // 4 + 1) * LANES] = low
            return carry

        lax.fori_loop(0, FRAME_ROWS // 16, fold, 0)

        section = dot3(one[0:256, :], one[256:512, :], fold_high[...], fold_low[...], ((1,), (0,)))
        cos_mid, sin_mid = mid[0:128, :], mid[128:256, :]
        for g in range(2):
            re = section[0:128, g * LANES : (g + 1) * LANES]
            im = section[128:256, g * LANES : (g + 1) * LANES]
            for part, value in enumerate((re * cos_mid + im * sin_mid, im * cos_mid - re * sin_mid)):
                high, low = halves(value)
                turn_high[g * 128 : (g + 1) * 128, part * LANES : (part + 1) * LANES] = high
                turn_low[g * 128 : (g + 1) * 128, part * LANES : (part + 1) * LANES] = low

        out = dot3(two[0:256, :], two[256:512, :], turn_high[...], turn_low[...], ((1,), (1,)))
        for part in range(2):
            for half in range(2):
                for side in range(2):
                    tiles = [
                        out[part * 128 + (half * 4 + q) * 16 : part * 128 + (half * 4 + q + 1) * 16,
                            side * LANES : (side + 1) * LANES]
                        for q in range(4)
                    ]
                    for r, tile in enumerate(exchange(tiles)):
                        staged[sub, part, half, pl.ds(side * 4 + r, 16, stride=8), :] = tile

    def step_body(i, carry):
        step = lax.rem(i + first_step, steps)

        @pl.when(i == 1)
        def _():
            for copy in late:
                copy.wait()

        @pl.when(jnp.logical_and(i == steps - first_step, me > 0))
        def _():
            rim_copy().wait_recv()

        for sub in range(2):
            eight_frames(step * STEP + sub * 8, sub)

        rows = pl.ds(pl.multiple_of(step * STEP, STEP), STEP)
        for c in range(PEERS):
            for part in range(2):
                for half in range(2):
                    pair = [staged[sub, part, half, c * 8 : (c + 1) * 8, :] for sub in range(2)]
                    ready[c, part, rows, half * LANES : (half + 1) * LANES] = jnp.concatenate(pair, axis=0).astype(
                        jnp.bfloat16
                    )

        there = pl.ds(pl.multiple_of(me * frames + step * STEP, STEP), STEP)
        for index, (dz, dx) in enumerate(OFFSETS):
            target = peer(me, dz, dx)
            pltpu.make_async_remote_copy(
                ready.at[target, :, rows],
                o_ref.at[:, there],
                send_sem.at[index],
                recv_sem.at[index],
                device_id={"tm": target},
                device_id_type=MESH,
            ).start()
        pltpu.make_async_copy(ready.at[me, :, rows], o_ref.at[:, there], send_sem.at[len(OFFSETS)]).start()
        return carry

    lax.fori_loop(0, steps, step_body, 0)

    @pl.when(me < PEERS - 1)
    def _():
        rim_copy().wait_send()

    mine = pl.ds(pl.multiple_of(me * frames, STEP), frames)
    pltpu.make_async_copy(ready.at[me], o_ref.at[:, mine], send_sem.at[len(OFFSETS)]).wait()
    for index, (dz, dx) in enumerate(OFFSETS):
        target = peer(me, dz, dx)
        source = peer(me, -dz, dx)
        here = pl.ds(pl.multiple_of(source * frames, STEP), frames)
        whole = pltpu.make_async_remote_copy(
            ready.at[target],
            o_ref.at[:, here],
            send_sem.at[index],
            recv_sem.at[index],
            device_id={"tm": target},
            device_id_type=MESH,
        )
        whole.wait_send()
        whole.wait_recv()


def local(samples, prototype):
    block_len = samples.shape[1]
    frames = block_len // HOP
    rows = 2 * block_len // LANES
    x = samples.reshape(2, block_len // LANES, LANES).transpose(1, 0, 2).reshape(rows, LANES)
    h = jnp.repeat(prototype.reshape(TAPS * ROWS, LANES), 2, axis=0)
    one = jnp.concatenate([jnp.asarray(part) for part in first_matrix()], axis=0)
    two = jnp.concatenate([jnp.asarray(part) for part in second_matrix()], axis=0)
    mid = jnp.asarray(middle_tables())
    width = CHANNELS // PEERS

    def body(*refs):
        kernel(frames, *refs)

    return pl.pallas_call(
        body,
        out_shape=jax.ShapeDtypeStruct((2, PEERS * frames, width), jnp.bfloat16),
        in_specs=[pl.BlockSpec(memory_space=pltpu.HBM)] * 5,
        out_specs=pl.BlockSpec(memory_space=pltpu.HBM),
        scratch_shapes=[
            pltpu.VMEM((RIM_ROWS + rows, LANES), jnp.float32),
            pltpu.VMEM((TAPS * FRAME_ROWS, LANES), jnp.float32),
            pltpu.VMEM((512, 256), jnp.bfloat16),
            pltpu.VMEM((256, LANES), jnp.float32),
            pltpu.VMEM((512, 256), jnp.bfloat16),
            pltpu.VMEM((256, 256), jnp.bfloat16),
            pltpu.VMEM((256, 256), jnp.bfloat16),
            pltpu.VMEM((256, 256), jnp.bfloat16),
            pltpu.VMEM((256, 256), jnp.bfloat16),
            pltpu.VMEM((2, 2, 2, 128, LANES), jnp.float32),
            pltpu.VMEM((PEERS, 2, frames, width), jnp.bfloat16),
            pltpu.SemaphoreType.DMA((7,)),
            pltpu.SemaphoreType.DMA((2,)),
            pltpu.SemaphoreType.DMA((len(OFFSETS) + 1,)),
            pltpu.SemaphoreType.DMA((len(OFFSETS),)),
        ],
        compiler_params=pltpu.CompilerParams(
            collective_id=0, has_side_effects=True, vmem_limit_bytes=60 * 1024 * 1024
        ),
    )(x, h, one, mid, two)


def solution(mesh):
    placed = (P(None, ("beam", "tm")), P())
    return jax.shard_map(
        local, mesh=mesh, in_specs=placed, out_specs=P(None, "beam", "tm"), check_vma=False
    )
```

profile of v0, /device:TPU:4, one launch (start us, length us, event | category | flops | bytes accessed | tf_op | source)
XLA Modules:
  0.0 94.7 jit_solution(12374789328238980895)
XLA Ops:
  0.0 1.0 %reshape.14 = f32[512,128]{1,0:T(8,128)S(1)} reshape(f32[16,4096]{1,0:T(8,128)} %param.8) | data formatting | bytes 524288 | tf_op jit(solution)/shard_map/reshape | solution.py:252
  1.0 1.0 %broadcast_in_dim.3 = f32[512,2,128]{2,1,0:T(2,128)} broadcast(f32[512,128]{1,0:T(8,128)S(1)} %reshape.14), dimensions={0,2} | broadcast | bytes 786432 | tf_op jit(solution)/shard_map/broadcast_in_dim | solution.py:252
  2.0 88.9 %shard_map.73 = bf16[2,3072,256]{2,1,0:T(8,128)(2,1)} custom-call(f32[9216,128]{1,0:T(8,128)} %bitcast.6, f32[1024,128]{1,0:T(8,128)} %bitcast.7, bf16[512,256]{1,0:T(8,128)(2,1)} %constant.15.refs_2_, f32[256,128]{1,0:T(8,128)} %constant.14.clone.refs_3_, bf16[512,256]{1,0:T(8,128)(2,1)} %constant.16.refs_4_), custom_call_target="tpu_custom_call" | custom-call | tf_op jit(solution)/shard_map/pallas_call | solution.py:261
  90.9 3.8 %copy.10 = bf16[2,3072,256]{2,1,0:T(8,128)(2,1)} copy(bf16[2,3072,256]{2,1,0:T(8,128)(2,1)} %shard_map.73) | data formatting | bytes 6291456
where the time goes:
time: 94.8 us; the launch traced here: 94.7 us
  Pallas kernels  88.9 us (94%)
  local copies, waits for them, and re-layouts  5.73 us (6%)
    pallas_call x1, Pallas kernels, local(): pl.pallas_call(body, out_shape=jax.ShapeDtypeStruct((2, PEERS * frames, w...  88.9 us
    unnamed x1, local copies, waits for them, and re-layouts  3.76 us

commit v1 on v0

--- a/solution.py
+++ b/solution.py
@@ -19,7 +19,7 @@
 RIM_ROWS = 2 * (TAPS * CHANNELS - HOP) // LANES
 STEP = 16
 MESH = pl.DeviceIdType.MESH
-OFFSETS = [(dz, dx) for dz in (1, -1, 2, -2, 3, -3, 4) for dx in (0, 1)] + [(0, 1)]
+OFFSETS = [(dz, dx) for dz in (4, 3, -3, 2, -2, 1, -1) for dx in (1, 0)] + [(0, 1)]
 
 
 def split_bf16(table):
@@ -73,7 +73,7 @@
 
 def kernel(
     frames, x_hbm, h_hbm, one_hbm, mid_hbm, two_hbm, o_ref,
-    x, h, one, mid, two, fold_high, fold_low, turn_high, turn_low, staged, ready,
+    x, rim_relay, taps_in, h, one, mid, two, fold_high, fold_low, turn_high, turn_low, staged, ready,
     load_sem, rim_sem, send_sem, recv_sem,
 ):
     me = lax.axis_index("tm")
@@ -94,7 +94,7 @@
 
     early = [
         load(0, low_row, high_row),
-        pltpu.make_async_copy(h_hbm, h, load_sem.at[3]),
+        pltpu.make_async_copy(h_hbm, taps_in, load_sem.at[3]),
         pltpu.make_async_copy(one_hbm, one, load_sem.at[4]),
         pltpu.make_async_copy(mid_hbm, mid, load_sem.at[5]),
         pltpu.make_async_copy(two_hbm, two, load_sem.at[6]),
@@ -103,28 +103,46 @@
     for copy in early + late:
         copy.start()
 
-    pl.semaphore_wait(barrier, len(OFFSETS))
-
-    def rim_copy():
+    half_rim = RIM_ROWS // 2
+    rim_start = local_rows - RIM_ROWS
+
+    def rim(index, source, place, steps_on):
         return pltpu.make_async_remote_copy(
-            x_hbm.at[pl.ds(local_rows - RIM_ROWS, RIM_ROWS)],
-            x.at[pl.ds(0, RIM_ROWS)],
-            rim_sem.at[0],
-            rim_sem.at[1],
-            device_id={"tm": lax.rem(me + 1, PEERS)},
+            source,
+            place,
+            rim_sem.at[0, index],
+            rim_sem.at[1, index],
+            device_id={"tm": lax.rem(me + steps_on + PEERS, PEERS)},
             device_id_type=MESH,
         )
 
-    @pl.when(me < PEERS - 1)
-    def _():
-        rim_copy().start()
-
-    @pl.when(me == 0)
-    def _():
-        x[pl.ds(0, RIM_ROWS), :] = jnp.zeros((RIM_ROWS, LANES), jnp.float32)
+    rim_whole = rim(0, x_hbm.at[pl.ds(rim_start, RIM_ROWS)], x.at[pl.ds(0, RIM_ROWS)], 1)
+    rim_direct = rim(1, x_hbm.at[pl.ds(rim_start, half_rim)], x.at[pl.ds(0, half_rim)], 1)
+    rim_aside = rim(2, x_hbm.at[pl.ds(rim_start + half_rim, half_rim)], rim_relay, -1)
+    rim_onward = rim(3, rim_relay, x.at[pl.ds(half_rim, half_rim)], 2)
+    odd = lax.rem(me, 2) == 1
+    even = lax.rem(me, 2) == 0
+    odd_sends = jnp.logical_and(odd, me < PEERS - 1)
+    even_relays = jnp.logical_and(even, me < PEERS - 2)
+    even_gets = jnp.logical_and(even, me > 0)
+
+    pl.semaphore_wait(barrier, len(OFFSETS))
+
+    @pl.when(even)
+    def _():
+        rim_whole.start()
+
+    @pl.when(odd_sends)
+    def _():
+        rim_direct.start()
+        rim_aside.start()
 
     for copy in early:
         copy.wait()
+
+    for a in range(ROWS):
+        for part in range(2):
+            h[pl.ds(2 * a + part, TAPS, stride=FRAME_ROWS), :] = taps_in[:, a * LANES : (a + 1) * LANES]
 
     lane = lax.broadcasted_iota(jnp.int32, (16, LANES), 1)
     low_64 = lane < 64
@@ -182,18 +200,7 @@
                     for r, tile in enumerate(exchange(tiles)):
                         staged[sub, part, half, pl.ds(side * 4 + r, 16, stride=8), :] = tile
 
-    def step_body(i, carry):
-        step = lax.rem(i + first_step, steps)
-
-        @pl.when(i == 1)
-        def _():
-            for copy in late:
-                copy.wait()
-
-        @pl.when(jnp.logical_and(i == steps - first_step, me > 0))
-        def _():
-            rim_copy().wait_recv()
-
+    def compute(step):
         for sub in range(2):
             eight_frames(step * STEP + sub * 8, sub)
 
@@ -206,6 +213,8 @@
                         jnp.bfloat16
                     )
 
+    def send(step):
+        rows = pl.ds(pl.multiple_of(step * STEP, STEP), STEP)
         there = pl.ds(pl.multiple_of(me * frames + step * STEP, STEP), STEP)
         for index, (dz, dx) in enumerate(OFFSETS):
             target = peer(me, dz, dx)
@@ -218,13 +227,53 @@
                 device_id_type=MESH,
             ).start()
         pltpu.make_async_copy(ready.at[me, :, rows], o_ref.at[:, there], send_sem.at[len(OFFSETS)]).start()
+
+    compute(first_step)
+    send(first_step)
+
+    @pl.when(me == 0)
+    def _():
+        x[pl.ds(0, RIM_ROWS), :] = jnp.zeros((RIM_ROWS, LANES), jnp.float32)
+
+    for copy in late:
+        copy.wait()
+
+    def step_body(i, carry):
+        step = lax.rem(i + first_step, steps)
+
+        @pl.when(jnp.logical_and(i == steps - first_step, odd))
+        def _():
+            rim_whole.wait_recv()
+
+        @pl.when(jnp.logical_and(i == steps - first_step, even_gets))
+        def _():
+            rim_direct.wait_recv()
+            rim_onward.wait_recv()
+
+        compute(step)
+
+        @pl.when(jnp.logical_and(i == 4, even_relays))
+        def _():
+            rim_aside.wait_recv()
+            rim_onward.start()
+
+        send(step)
         return carry
 
-    lax.fori_loop(0, steps, step_body, 0)
-
-    @pl.when(me < PEERS - 1)
-    def _():
-        rim_copy().wait_send()
+    lax.fori_loop(1, steps, step_body, 0)
+
+    @pl.when(even)
+    def _():
+        rim_whole.wait_send()
+
+    @pl.when(odd_sends)
+    def _():
+        rim_direct.wait_send()
+        rim_aside.wait_send()
+
+    @pl.when(even_relays)
+    def _():
+        rim_onward.wait_send()
 
     mine = pl.ds(pl.multiple_of(me * frames, STEP), frames)
     pltpu.make_async_copy(ready.at[me], o_ref.at[:, mine], send_sem.at[len(OFFSETS)]).wait()
@@ -249,7 +298,6 @@
     frames = block_len // HOP
     rows = 2 * block_len // LANES
     x = samples.reshape(2, block_len // LANES, LANES).transpose(1, 0, 2).reshape(rows, LANES)
-    h = jnp.repeat(prototype.reshape(TAPS * ROWS, LANES), 2, axis=0)
     one = jnp.concatenate([jnp.asarray(part) for part in first_matrix()], axis=0)
     two = jnp.concatenate([jnp.asarray(part) for part in second_matrix()], axis=0)
     mid = jnp.asarray(middle_tables())
@@ -265,6 +313,8 @@
         out_specs=pl.BlockSpec(memory_space=pltpu.HBM),
         scratch_shapes=[
             pltpu.VMEM((RIM_ROWS + rows, LANES), jnp.float32),
+            pltpu.VMEM((RIM_ROWS // 2, LANES), jnp.float32),
+            pltpu.VMEM((TAPS, CHANNELS), jnp.float32),
             pltpu.VMEM((TAPS * FRAME_ROWS, LANES), jnp.float32),
             pltpu.VMEM((512, 256), jnp.bfloat16),
             pltpu.VMEM((256, LANES), jnp.float32),
@@ -276,14 +326,14 @@
             pltpu.VMEM((2, 2, 2, 128, LANES), jnp.float32),
             pltpu.VMEM((PEERS, 2, frames, width), jnp.bfloat16),
             pltpu.SemaphoreType.DMA((7,)),
-            pltpu.SemaphoreType.DMA((2,)),
+            pltpu.SemaphoreType.DMA((2, 4)),
             pltpu.SemaphoreType.DMA((len(OFFSETS) + 1,)),
             pltpu.SemaphoreType.DMA((len(OFFSETS),)),
         ],
         compiler_params=pltpu.CompilerParams(
-            collective_id=0, has_side_effects=True, vmem_limit_bytes=60 * 1024 * 1024
+            collective_id=0, has_side_effects=True, vmem_limit_bytes=40 * 1024 * 1024
         ),
-    )(x, h, one, mid, two)
+    )(*[pltpu.with_memory_space_constraint(value, pltpu.HBM) for value in (x, prototype, one, mid, two)])
 
 
 def solution(mesh):

time: 94.8 us -> 86.9 us (0.917)
  Pallas kernels: 88.9 us -> 84.8 us
  local copies, waits for them, and re-layouts: 5.73 us -> 1.67 us
    pallas_call x1, Pallas kernels: 88.9 us -> 84.8 us  [local(): pl.pallas_call(body, out_shape=jax.ShapeDtypeStruct((2, PEERS * frames, w...]
    unnamed x1, local copies, waits for them, and re-layouts: 3.76 us -> 1.67 us
    reshape x1 -> x0, local copies, waits for them, and re-layouts: 1 us -> none  [local(): h = jnp.repeat(prototype.reshape(TAPS * ROWS, LANES), 2, axis=0)]
    broadcast_in_dim x1 -> x0, local copies, waits for them, and re-layouts: 0.97 us -> none  [local(): h = jnp.repeat(prototype.reshape(TAPS * ROWS, LANES), 2, axis=0)]
where the time goes in v1:
time: 86.9 us; the launch traced here: 86.4 us
  Pallas kernels  84.8 us (98%)
  local copies, waits for them, and re-layouts  1.67 us (2%)
    pallas_call x1, Pallas kernels, local(): pl.pallas_call(body, out_shape=jax.ShapeDtypeStruct((2, PEERS * frames, w...  84.8 us

profile of v1, /device:TPU:4, one launch (start us, length us, event | category | flops | bytes accessed | tf_op | source)
XLA Modules:
  0.0 86.4 jit_solution(11416101627523687699)
XLA Ops:
  0.0 84.8 %shard_map.73 = bf16[2,3072,256]{2,1,0:T(8,128)(2,1)S(1)} custom-call(f32[9216,128]{1,0:T(8,128)} %bitcast.5, f32[16,4096]{1,0:T(8,128)} %refs_1_.1, bf16[512,256]{1,0:T(8,128)(2,1)} %constant.15.refs_2_, f32[256,128]{1,0:T(8,128)} %constant.14.clone.refs_3_, bf16[512,256]{1,0:T(8,128)(2,1)} %constant.16.refs_4_), custom_call_target="tpu_custom_call" | custom-call | tf_op jit(solution)/shard_map/pallas_call | solution.py:309
  84.8 1.7 %copy.10 = bf16[2,3072,256]{2,1,0:T(8,128)(2,1)} copy(bf16[2,3072,256]{2,1,0:T(8,128)(2,1)S(1)} %shard_map.73) | data formatting | bytes 6291456

commit v2 on v1

--- a/solution.py
+++ b/solution.py
@@ -18,6 +18,7 @@
 HOP_ROWS = 2 * HOP // LANES
 RIM_ROWS = 2 * (TAPS * CHANNELS - HOP) // LANES
 STEP = 16
+ASIDE_FIRST, ASIDE_COUNT, ASIDE_ONWARD = 2, 2, 7
 MESH = pl.DeviceIdType.MESH
 OFFSETS = [(dz, dx) for dz in (4, 3, -3, 2, -2, 1, -1) for dx in (1, 0)] + [(0, 1)]
 
@@ -73,8 +74,8 @@
 
 def kernel(
     frames, x_hbm, h_hbm, one_hbm, mid_hbm, two_hbm, o_ref,
-    x, rim_relay, taps_in, h, one, mid, two, fold_high, fold_low, turn_high, turn_low, staged, ready,
-    load_sem, rim_sem, send_sem, recv_sem,
+    x, rim_relay, far_relay, taps_in, h, one, mid, two, fold_high, fold_low, turn_high, turn_low, staged, ready,
+    load_sem, rim_sem, far_sem, send_sem, recv_sem,
 ):
     me = lax.axis_index("tm")
     local_rows = frames * HOP_ROWS
@@ -125,17 +126,6 @@
     odd_sends = jnp.logical_and(odd, me < PEERS - 1)
     even_relays = jnp.logical_and(even, me < PEERS - 2)
     even_gets = jnp.logical_and(even, me > 0)
-
-    pl.semaphore_wait(barrier, len(OFFSETS))
-
-    @pl.when(even)
-    def _():
-        rim_whole.start()
-
-    @pl.when(odd_sends)
-    def _():
-        rim_direct.start()
-        rim_aside.start()
 
     for copy in early:
         copy.wait()
@@ -200,9 +190,11 @@
                     for r, tile in enumerate(exchange(tiles)):
                         staged[sub, part, half, pl.ds(side * 4 + r, 16, stride=8), :] = tile
 
-    def compute(step):
+    def compute(step, between=None):
         for sub in range(2):
             eight_frames(step * STEP + sub * 8, sub)
+            if sub == 0 and between is not None:
+                between()
 
         rows = pl.ds(pl.multiple_of(step * STEP, STEP), STEP)
         for c in range(PEERS):
@@ -213,22 +205,75 @@
                         jnp.bfloat16
                     )
 
-    def send(step):
+    def direct(step, index):
+        dz, dx = OFFSETS[index]
+        rows = pl.ds(pl.multiple_of(step * STEP, STEP), STEP)
+        target = peer(me, dz, dx)
+        return pltpu.make_async_remote_copy(
+            ready.at[target, :, rows],
+            o_ref.at[:, pl.ds(pl.multiple_of(me * frames + step * STEP, STEP), STEP)],
+            send_sem.at[index],
+            recv_sem.at[index],
+            device_id={"tm": target},
+            device_id_type=MESH,
+        )
+
+    z_even = lax.rem(me // 2, 2) == 0
+    z_odd = lax.rem(me // 2, 2) == 1
+
+    def far_aside(step, slot, dx):
+        rows = pl.ds(pl.multiple_of(step * STEP, STEP), STEP)
+        return pltpu.make_async_remote_copy(
+            ready.at[peer(me, 4, dx), :, rows],
+            far_relay.at[slot, dx],
+            send_sem.at[OFFSETS.index((4, dx))],
+            far_sem.at[1, slot, dx],
+            device_id={"tm": peer(me, -1, 0)},
+            device_id_type=MESH,
+        )
+
+    def far_onward(slot, dx):
+        source = peer(me, 1, 0)
+        step = slot + ASIDE_FIRST + first_step
+        return pltpu.make_async_remote_copy(
+            far_relay.at[slot, dx],
+            o_ref.at[:, pl.ds(pl.multiple_of(source * frames + step * STEP, STEP), STEP)],
+            far_sem.at[0, slot, dx],
+            recv_sem.at[OFFSETS.index((4, dx))],
+            device_id={"tm": peer(me, -3, dx)},
+            device_id_type=MESH,
+        )
+
+    def send(step, aside=None):
+        for index, (dz, dx) in enumerate(OFFSETS):
+            if dz == 4 and aside is not None:
+                for slot in range(ASIDE_COUNT):
+                    @pl.when(jnp.logical_and(aside == slot, z_even))
+                    def _():
+                        far_aside(step, slot, dx).start()
+
+                @pl.when(jnp.logical_or(jnp.logical_or(aside < 0, aside >= ASIDE_COUNT), z_odd))
+                def _():
+                    direct(step, index).start()
+            else:
+                direct(step, index).start()
         rows = pl.ds(pl.multiple_of(step * STEP, STEP), STEP)
         there = pl.ds(pl.multiple_of(me * frames + step * STEP, STEP), STEP)
-        for index, (dz, dx) in enumerate(OFFSETS):
-            target = peer(me, dz, dx)
-            pltpu.make_async_remote_copy(
-                ready.at[target, :, rows],
-                o_ref.at[:, there],
-                send_sem.at[index],
-                recv_sem.at[index],
-                device_id={"tm": target},
-                device_id_type=MESH,
-            ).start()
         pltpu.make_async_copy(ready.at[me, :, rows], o_ref.at[:, there], send_sem.at[len(OFFSETS)]).start()
 
-    compute(first_step)
+    def meet():
+        pl.semaphore_wait(barrier, len(OFFSETS))
+
+        @pl.when(even)
+        def _():
+            rim_whole.start()
+
+        @pl.when(odd_sends)
+        def _():
+            rim_direct.start()
+            rim_aside.start()
+
+    compute(first_step, meet)
     send(first_step)
 
     @pl.when(me == 0)
@@ -257,7 +302,14 @@
             rim_aside.wait_recv()
             rim_onward.start()
 
-        send(step)
+        @pl.when(jnp.logical_and(i == ASIDE_ONWARD, z_odd))
+        def _():
+            for slot in range(ASIDE_COUNT):
+                for dx in range(2):
+                    far_aside(step, slot, dx).wait_recv()
+                    far_onward(slot, dx).start()
+
+        send(step, i - ASIDE_FIRST)
         return carry
 
     lax.fori_loop(1, steps, step_body, 0)
@@ -274,6 +326,12 @@
     @pl.when(even_relays)
     def _():
         rim_onward.wait_send()
+
+    @pl.when(z_odd)
+    def _():
+        for slot in range(ASIDE_COUNT):
+            for dx in range(2):
+                far_onward(slot, dx).wait_send()
 
     mine = pl.ds(pl.multiple_of(me * frames, STEP), frames)
     pltpu.make_async_copy(ready.at[me], o_ref.at[:, mine], send_sem.at[len(OFFSETS)]).wait()
@@ -314,6 +372,7 @@
         scratch_shapes=[
             pltpu.VMEM((RIM_ROWS + rows, LANES), jnp.float32),
             pltpu.VMEM((RIM_ROWS // 2, LANES), jnp.float32),
+            pltpu.VMEM((ASIDE_COUNT, 2, 2, STEP, width), jnp.bfloat16),
             pltpu.VMEM((TAPS, CHANNELS), jnp.float32),
             pltpu.VMEM((TAPS * FRAME_ROWS, LANES), jnp.float32),
             pltpu.VMEM((512, 256), jnp.bfloat16),
@@ -327,6 +386,7 @@
             pltpu.VMEM((PEERS, 2, frames, width), jnp.bfloat16),
             pltpu.SemaphoreType.DMA((7,)),
             pltpu.SemaphoreType.DMA((2, 4)),
+            pltpu.SemaphoreType.DMA((2, ASIDE_COUNT, 2)),
             pltpu.SemaphoreType.DMA((len(OFFSETS) + 1,)),
             pltpu.SemaphoreType.DMA((len(OFFSETS),)),
         ],

time: 86.9 us -> 83.5 us (0.961)
  Pallas kernels: 84.8 us -> 81.5 us
    pallas_call x1, Pallas kernels: 84.8 us -> 81.5 us  [local(): pl.pallas_call(body, out_shape=jax.ShapeDtypeStruct((2, PEERS * frames, w...]
where the time goes in v2:
time: 83.5 us; the launch traced here: 83.1 us
  Pallas kernels  81.5 us (98%)
  local copies, waits for them, and re-layouts  1.67 us (2%)
    pallas_call x1, Pallas kernels, local(): pl.pallas_call(body, out_shape=jax.ShapeDtypeStruct((2, PEERS * frames, w...  81.5 us

profile of v2, /device:TPU:4, one launch (start us, length us, event | category | flops | bytes accessed | tf_op | source)
XLA Modules:
  0.0 83.1 jit_solution(13962768200120399548)
XLA Ops:
  0.0 81.5 %shard_map.73 = bf16[2,3072,256]{2,1,0:T(8,128)(2,1)S(1)} custom-call(f32[9216,128]{1,0:T(8,128)} %bitcast.5, f32[16,4096]{1,0:T(8,128)} %refs_1_.1, bf16[512,256]{1,0:T(8,128)(2,1)} %constant.15.refs_2_, f32[256,128]{1,0:T(8,128)} %constant.14.clone.refs_3_, bf16[512,256]{1,0:T(8,128)(2,1)} %constant.16.refs_4_), custom_call_target="tpu_custom_call" | custom-call | tf_op jit(solution)/shard_map/pallas_call | solution.py:367
  81.5 1.7 %copy.10 = bf16[2,3072,256]{2,1,0:T(8,128)(2,1)} copy(bf16[2,3072,256]{2,1,0:T(8,128)(2,1)S(1)} %shard_map.73) | data formatting | bytes 6291456

commit v3 on v2

--- a/solution.py
+++ b/solution.py
@@ -18,7 +18,7 @@
 HOP_ROWS = 2 * HOP // LANES
 RIM_ROWS = 2 * (TAPS * CHANNELS - HOP) // LANES
 STEP = 16
-ASIDE_FIRST, ASIDE_COUNT, ASIDE_ONWARD = 2, 2, 7
+ASIDE_FIRST, ASIDE_COUNT, ASIDE_ONWARD = 5, 2, 9
 MESH = pl.DeviceIdType.MESH
 OFFSETS = [(dz, dx) for dz in (4, 3, -3, 2, -2, 1, -1) for dx in (1, 0)] + [(0, 1)]
 
@@ -245,7 +245,10 @@
         )
 
     def send(step, aside=None):
-        for index, (dz, dx) in enumerate(OFFSETS):
+        order = list(enumerate(OFFSETS))
+        if aside is None:
+            order.reverse()
+        for index, (dz, dx) in order:
             if dz == 4 and aside is not None:
                 for slot in range(ASIDE_COUNT):
                     @pl.when(jnp.logical_and(aside == slot, z_even))

time: 83.5 us -> 83.4 us (level)
  no operation moved by 1% of the time
where the time goes in v3:
time: 83.4 us; the launch traced here: 83.1 us
  Pallas kernels  81.4 us (98%)
  local copies, waits for them, and re-layouts  1.67 us (2%)
    pallas_call x1, Pallas kernels, local(): pl.pallas_call(body, out_shape=jax.ShapeDtypeStruct((2, PEERS * frames, w...  81.4 us

profile of v3, /device:TPU:4, one launch (start us, length us, event | category | flops | bytes accessed | tf_op | source)
XLA Modules:
  0.0 83.1 jit_solution(5343810651286706122)
XLA Ops:
  0.0 81.4 %shard_map.73 = bf16[2,3072,256]{2,1,0:T(8,128)(2,1)S(1)} custom-call(f32[9216,128]{1,0:T(8,128)} %bitcast.5, f32[16,4096]{1,0:T(8,128)} %refs_1_.1, bf16[512,256]{1,0:T(8,128)(2,1)} %constant.15.refs_2_, f32[256,128]{1,0:T(8,128)} %constant.14.clone.refs_3_, bf16[512,256]{1,0:T(8,128)(2,1)} %constant.16.refs_4_), custom_call_target="tpu_custom_call" | custom-call | tf_op jit(solution)/shard_map/pallas_call | solution.py:370
  81.4 1.7 %copy.10 = bf16[2,3072,256]{2,1,0:T(8,128)(2,1)} copy(bf16[2,3072,256]{2,1,0:T(8,128)(2,1)S(1)} %shard_map.73) | data formatting | bytes 6291456
